TPU v7x, 32 devices: a whole 2x2x4 slice. The times are simulated.
32 devices in a mesh: gx: 4 (over x, core), gy: 8 (over z, y).
Axes of the slice: x: 2, y: 2, z: 4, core: 2. Of those that a mesh axis runs over, the one named last changes fastest.
Arguments:
- electric: float32 [3, 64, 128, 256], P(None, 'gx', 'gy'), may hold values from -6 to 6
- magnetic: float32 [3, 64, 128, 256], P(None, 'gx', 'gy'), may hold values from -6 to 6
- aux_electric: float32 [6, 64, 128, 256], P(None, 'gx', 'gy'), may hold values from -3 to 3
- aux_magnetic: float32 [6, 64, 128, 256], P(None, 'gx', 'gy'), may hold values from -3 to 3
- grades: int32 [3, 64, 128, 256], P(None, 'gx', 'gy'), may hold values from 0 to 3
- permittivity: float32 [64, 128, 256], P('gx', 'gy'), may hold values from 1 to 8
- dipole_cell: int32 [3, 16384], P(None, ('gx', 'gy')), may hold values from 0 to 255, as said below
- dipole_port: int32 [16384], P(('gx', 'gy')), may hold values from 0 to 511
- live_count: int32 [32], P(('gx', 'gy')), may hold values from 1 to 512, as said below
- injection: bfloat16 [16384, 512], P(('gx', 'gy')), may hold values from -0.25 to 0.25
- waveform: bfloat16 [512, 16], replicated, may hold values from -6 to 6
Outputs:
- electric_out: float32 [3, 64, 128, 256], P(None, 'gx', 'gy')
- magnetic_out: float32 [3, 64, 128, 256], P(None, 'gx', 'gy')
- port_power: float32 [16, 512], replicated
Inputs may be any that keep to these rules, and one draw needn't show every extreme that they name: `dipole_cell`: slot s lies in the block of cells held by the device that holds slot s. The live slots of a device are its first live_count ones; some device has all 512 live.
All inputs are finite; a program needn't handle non-finite values.
Results may differ from a plain program's by a relative error of at most 0.0003.
Values sent between devices are 32-bit elements; how exact they have to be, the bound alone decides.
No kernel may reach another device: no remote copies, remote signals or barrier semaphores. Data moves between devices by JAX's collectives and lax.ppermute only.
A program may use at most 128 MiB of HBM per device.

v0:
```python
import jax
import jax.numpy as jnp
from jax import lax
from jax.sharding import PartitionSpec as P

courant = 0.55
absorb_keep = (0.0, 0.92, 0.75, 0.45)
absorb_take = (0.0, -0.06, -0.18, -0.35)
derivative_pairs = ((2, 1), (1, 2), (0, 2), (2, 0), (1, 0), (0, 1))


def passed_along(block, axis, distance):
    devices = range(lax.axis_size(axis))
    route = [(i - distance, i) for i in devices if i - distance in devices]
    return lax.ppermute(block, axis, route)


def difference(values, axis, plane, forward):
    length = values.shape[axis]
    if plane is None:
        shape = list(values.shape)
        shape[axis] = 1
        plane = jnp.zeros(shape, values.dtype)
    if forward:
        after = jnp.concatenate([lax.slice_in_dim(values, 1, length, axis=axis), plane], axis)
        return after - values
    before = jnp.concatenate([plane, lax.slice_in_dim(values, 0, length - 1, axis=axis)], axis)
    return values - before


def grade_table(grades, table):
    result = jnp.zeros(grades.shape, jnp.float32)
    for level in range(1, 4):
        result = result + jnp.where(grades == level, table[level], 0.0)
    return result


def curl_parts(field, auxiliary, keep, take, planes, forward):
    terms = []
    updated = []
    for number, (component, axis) in enumerate(derivative_pairs):
        plane = None
        if planes is not None and axis == 0:
            plane = planes[0][component - 1]
        if planes is not None and axis == 1:
            plane = planes[1][component // 2]
        slope = difference(field[component], axis, plane, forward)
        carried = keep[axis] * auxiliary[number] + take[axis] * slope
        terms.append(slope + carried)
        updated.append(carried)
    rotation = (terms[0] - terms[1], terms[2] - terms[3], terms[4] - terms[5])
    return (rotation, tuple(updated))


def inject(z_plane, current_now, cell_table, depth_table):
    weighted = cell_table * current_now[:, None]
    source = lax.dot_general(
        weighted, depth_table, (((0,), (0,)), ((), ())), precision=lax.Precision.HIGHEST
    )
    return z_plane - courant * source.reshape(z_plane.shape)


def read_cells(z_plane, cell_table, depth_table):
    rows = z_plane.reshape(cell_table.shape[1], depth_table.shape[1])
    picked = jnp.dot(cell_table, rows, precision=lax.Precision.HIGHEST)
    return jnp.sum(picked * depth_table, axis=1)


def note_power(record, drive, index):
    return lax.dynamic_update_slice_in_dim(record, drive[None, :], index, 0)


def local(
    electric,
    magnetic,
    aux_electric,
    aux_magnetic,
    grades,
    permittivity,
    dipole_cell,
    dipole_port,
    live_count,
    injection,
    waveform,
):
    depth_x, depth_y, depth_z = electric.shape[1:]
    slots = dipole_cell.shape[1]
    ports, steps = waveform.shape
    row_index = lax.axis_index("gx")
    col_index = lax.axis_index("gy")
    plane_cell = (dipole_cell[0] - row_index * depth_x) * depth_y + (
        dipole_cell[1] - col_index * depth_y
    )
    cell_table = (
        plane_cell[:, None] == jnp.arange(depth_x * depth_y, dtype=jnp.int32)[None, :]
    ).astype(jnp.float32)
    depth_table = (dipole_cell[2][:, None] == jnp.arange(depth_z, dtype=jnp.int32)[None, :]).astype(
        jnp.float32
    )
    live = (jnp.arange(slots, dtype=jnp.int32) < live_count[0]).astype(jnp.float32)
    current = jnp.dot(injection, waveform, preferred_element_type=jnp.float32) * live[:, None]
    members = (dipole_port[:, None] == jnp.arange(ports, dtype=jnp.int32)[None, :]).astype(
        jnp.float32
    )
    factor = courant / permittivity
    keep = grade_table(grades, absorb_keep)
    take = grade_table(grades, absorb_take)
    record = jnp.zeros((steps, slots), jnp.float32)

    def turn_parts(step, carry):
        field_e, field_h, memory_e, memory_h, record = carry
        next_x = passed_along(jnp.stack([field_e[1][0:1], field_e[2][0:1]]), "gx", -1)
        next_y = passed_along(jnp.stack([field_e[0][:, 0:1], field_e[2][:, 0:1]]), "gy", -1)
        rotation, memory_e = curl_parts(field_e, memory_e, keep, take, (next_x, next_y), True)
        field_h = tuple((field_h[number] - courant * rotation[number] for number in range(3)))
        prior_x = passed_along(jnp.stack([field_h[1][-1:], field_h[2][-1:]]), "gx", 1)
        prior_y = passed_along(jnp.stack([field_h[0][:, -1:], field_h[2][:, -1:]]), "gy", 1)
        rotation, memory_h = curl_parts(field_h, memory_h, keep, take, (prior_x, prior_y), False)
        current_now = lax.dynamic_slice_in_dim(current, step, 1, 1)[:, 0]
        z_plane = inject(field_e[2] + factor * rotation[2], current_now, cell_table, depth_table)
        field_e = (field_e[0] + factor * rotation[0], field_e[1] + factor * rotation[1], z_plane)
        drive = current_now * read_cells(z_plane, cell_table, depth_table)
        record = note_power(record, drive, step)
        return (field_e, field_h, memory_e, memory_h, record)

    start_state = (
        tuple((electric[number] for number in range(3))),
        tuple((magnetic[number] for number in range(3))),
        tuple((aux_electric[number] for number in range(6))),
        tuple((aux_magnetic[number] for number in range(6))),
        record,
    )
    parts_e, parts_h, parts_me, parts_mh, record = lax.fori_loop(0, steps, turn_parts, start_state)
    electric = jnp.stack(parts_e)
    magnetic = jnp.stack(parts_h)
    partial_value = jnp.dot(record, members, precision=lax.Precision.HIGHEST)
    port_power = lax.psum(partial_value, ("gx", "gy"))
    return (electric, magnetic, port_power)


def solution(mesh):
    in_specs = (
        P(None, "gx", "gy", None),
        P(None, "gx", "gy", None),
        P(None, "gx", "gy", None),
        P(None, "gx", "gy", None),
        P(None, "gx", "gy", None),
        P("gx", "gy", None),
        P(None, ("gx", "gy")),
        P(("gx", "gy")),
        P(("gx", "gy")),
        P(("gx", "gy"), None),
        P(),
    )
    out_specs = (P(None, "gx", "gy", None), P(None, "gx", "gy", None), P())
    return jax.shard_map(local, mesh=mesh, in_specs=in_specs, out_specs=out_specs, check_vma=False)
```

profile of v0, /device:TPU:0, one launch (start us, length us, event | category | flops | bytes accessed | tf_op | source)
XLA Modules:
  0.0 605.0 jit_solution(2541762445763992828)
XLA Ops:
  10.5 545.4 %while.50 = (s32[]{:T(128)}, f32[16,16,256]{2,1,0:T(8,128)S(1)}, f32[16,16,256]{2,1,0:T(8,128)S(1)}, f32[16,16,256]{2,1,0:T(8,128)S(1)}, f32[16,16,256]{2,1,0:T(...) while((s32[]{:T(128)}, f32[16,16,256]{2,1,0:T(8,128)S(1)}, ...), condition=%wide.region_2.3_spmd.clone, body=%wide.region_0.2_spmd.clone.sunk | while | flops 812285952 | bytes 56044672 | solution.py:133
  20.5 2.4 multiply_subtract_fusion.7
  23.5 5.5 collective-permute-start.2
  30.9 2.8 collective-permute-start.3
  52.6 2.4 multiply_subtract_fusion.7
  55.6 5.4 collective-permute-start.2
  63.0 3.8 collective-permute-start.3
  85.7 2.4 multiply_subtract_fusion.7
  88.7 5.2 collective-permute-start.2
  95.8 5.3 collective-permute-start.3
  120.0 2.4 multiply_subtract_fusion.7
  123.0 5.2 collective-permute-start.2
  130.1 5.3 collective-permute-start.3
  154.3 2.4 multiply_subtract_fusion.7
  157.3 5.2 collective-permute-start.2
  164.4 5.3 collective-permute-start.3
  188.6 2.4 multiply_subtract_fusion.7
  191.6 5.2 collective-permute-start.2
  198.7 5.3 collective-permute-start.3
  222.9 2.4 multiply_subtract_fusion.7
  225.9 5.2 collective-permute-start.2
  233.0 5.3 collective-permute-start.3
  257.2 2.4 multiply_subtract_fusion.7
  260.2 5.2 collective-permute-start.2
  267.3 5.3 collective-permute-start.3
  291.5 2.4 multiply_subtract_fusion.7
  294.5 5.2 collective-permute-start.2
  301.6 5.3 collective-permute-start.3
  325.8 2.4 multiply_subtract_fusion.7
  328.8 5.2 collective-permute-start.2
  335.9 5.3 collective-permute-start.3
  360.1 2.4 multiply_subtract_fusion.7
  363.1 5.2 collective-permute-start.2
  370.2 5.3 collective-permute-start.3
  394.4 2.4 multiply_subtract_fusion.7
  397.4 5.2 collective-permute-start.2
  404.5 5.3 collective-permute-start.3
  428.7 2.4 multiply_subtract_fusion.7
  431.7 5.2 collective-permute-start.2
  438.8 5.3 collective-permute-start.3
  463.0 2.4 multiply_subtract_fusion.7
  466.0 5.2 collective-permute-start.2
  473.1 5.3 collective-permute-start.3
  500.3 5.2 collective-permute-start.2
  507.4 5.3 collective-permute-start.3
  534.6 5.2 collective-permute-start.2
  541.7 5.3 collective-permute-start.3
  557.2 45.9 %psum.7 = f32[16,512]{1,0:T(8,128)} all-reduce(f32[16,512]{1,0:T(8,128)S(1)} %fusion.27), channel_id=1, replica_groups=mesh['gx'=4,'gy'=8] {'gx','gy'}, use_global_device_ids=true, to_apply=%region_3.4 | all-reduce | flops 8192 | bytes 65536 | tf_op jit(solution)/shard_map/psum | solution.py:137
  (1470 shorter events, 352.0 us)
Async XLA Ops:
  10.6 9.9 %collective-permute-start.1 = (f32[2,16,1,256]{3,2,1,0:T(1,128)S(1)}, f32[2,16,1,256]{3,2,1,0:T(1,128)S(1)}, u32[]{:S(2)}, u32[]{:S(2)}) collective-permute-start(f32[2,16,1,256]{3,2,1,0:T(1,128)S(1)} %pad_maximum_fusion.11), channel_id=1, source_target_pairs={{1,0},{2,1},{3,2},{4,3},{5,4},{6,5},{7,6},{9,8},{10,9},{11,10},{12... | collective-permute-start | bytes 98312 | tf_op jit(solution)/shard_map/while/body/eval_jaxpr/ppermute | solution.py:15
  11.9 8.5 %collective-permute-start = (f32[2,1,16,256]{3,2,1,0:T(8,128)S(1)}, f32[2,1,16,256]{3,2,1,0:T(8,128)S(1)}, u32[]{:S(2)}, u32[]{:S(2)}) collective-permute-start(f32[2,1,16,256]{3,2,1,0:T(8,128)S(1)} %pad_maximum_fusion.10), channel_id=1, source_target_pairs={{8,0},{16,8},{24,16},{9,1},{17,9},{25,17},{10,2},{18,10},{26,18},{... | collective-permute-start | bytes 98312 | tf_op jit(solution)/shard_map/while/body/eval_jaxpr/ppermute | solution.py:15
  23.5 10.2 %collective-permute-start.2 = (f32[2,16,1,256]{3,2,1,0:T(1,128)S(1)}, f32[2,16,1,256]{3,2,1,0:T(1,128)S(1)}, u32[]{:S(2)}, u32[]{:S(2)}) collective-permute-start(f32[2,16,1,256]{3,2,1,0:T(1,128)S(1)} %pad_maximum_fusion.12), channel_id=1, source_target_pairs={{0,1},{1,2},{2,3},{3,4},{4,5},{5,6},{6,7},{8,9},{9,10},{10,11},{11... | collective-permute-start | bytes 98312 | tf_op jit(solution)/shard_map/while/body/eval_jaxpr/ppermute | solution.py:15
  42.7 9.9 %collective-permute-start.1 = (f32[2,16,1,256]{3,2,1,0:T(1,128)S(1)}, f32[2,16,1,256]{3,2,1,0:T(1,128)S(1)}, u32[]{:S(2)}, u32[]{:S(2)}) collective-permute-start(f32[2,16,1,256]{3,2,1,0:T(1,128)S(1)} %pad_maximum_fusion.11), channel_id=1, source_target_pairs={{1,0},{2,1},{3,2},{4,3},{5,4},{6,5},{7,6},{9,8},{10,9},{11,10},{12... | collective-permute-start | bytes 98312 | tf_op jit(solution)/shard_map/while/body/eval_jaxpr/ppermute | solution.py:15
  44.0 8.5 %collective-permute-start = (f32[2,1,16,256]{3,2,1,0:T(8,128)S(1)}, f32[2,1,16,256]{3,2,1,0:T(8,128)S(1)}, u32[]{:S(2)}, u32[]{:S(2)}) collective-permute-start(f32[2,1,16,256]{3,2,1,0:T(8,128)S(1)} %pad_maximum_fusion.10), channel_id=1, source_target_pairs={{8,0},{16,8},{24,16},{9,1},{17,9},{25,17},{10,2},{18,10},{26,18},{... | collective-permute-start | bytes 98312 | tf_op jit(solution)/shard_map/while/body/eval_jaxpr/ppermute | solution.py:15
  55.6 11.2 %collective-permute-start.2 = (f32[2,16,1,256]{3,2,1,0:T(1,128)S(1)}, f32[2,16,1,256]{3,2,1,0:T(1,128)S(1)}, u32[]{:S(2)}, u32[]{:S(2)}) collective-permute-start(f32[2,16,1,256]{3,2,1,0:T(1,128)S(1)} %pad_maximum_fusion.12), channel_id=1, source_target_pairs={{0,1},{1,2},{2,3},{3,4},{4,5},{5,6},{6,7},{8,9},{9,10},{10,11},{11... | collective-permute-start | bytes 98312 | tf_op jit(solution)/shard_map/while/body/eval_jaxpr/ppermute | solution.py:15
  75.8 9.9 %collective-permute-start.1 = (f32[2,16,1,256]{3,2,1,0:T(1,128)S(1)}, f32[2,16,1,256]{3,2,1,0:T(1,128)S(1)}, u32[]{:S(2)}, u32[]{:S(2)}) collective-permute-start(f32[2,16,1,256]{3,2,1,0:T(1,128)S(1)} %pad_maximum_fusion.11), channel_id=1, source_target_pairs={{1,0},{2,1},{3,2},{4,3},{5,4},{6,5},{7,6},{9,8},{10,9},{11,10},{12... | collective-permute-start | bytes 98312 | tf_op jit(solution)/shard_map/while/body/eval_jaxpr/ppermute | solution.py:15
  77.1 8.5 %collective-permute-start = (f32[2,1,16,256]{3,2,1,0:T(8,128)S(1)}, f32[2,1,16,256]{3,2,1,0:T(8,128)S(1)}, u32[]{:S(2)}, u32[]{:S(2)}) collective-permute-start(f32[2,1,16,256]{3,2,1,0:T(8,128)S(1)} %pad_maximum_fusion.10), channel_id=1, source_target_pairs={{8,0},{16,8},{24,16},{9,1},{17,9},{25,17},{10,2},{18,10},{26,18},{... | collective-permute-start | bytes 98312 | tf_op jit(solution)/shard_map/while/body/eval_jaxpr/ppermute | solution.py:15
  88.7 12.4 %collective-permute-start.2 = (f32[2,16,1,256]{3,2,1,0:T(1,128)S(1)}, f32[2,16,1,256]{3,2,1,0:T(1,128)S(1)}, u32[]{:S(2)}, u32[]{:S(2)}) collective-permute-start(f32[2,16,1,256]{3,2,1,0:T(1,128)S(1)} %pad_maximum_fusion.12), channel_id=1, source_target_pairs={{0,1},{1,2},{2,3},{3,4},{4,5},{5,6},{6,7},{8,9},{9,10},{10,11},{11... | collective-permute-start | bytes 98312 | tf_op jit(solution)/shard_map/while/body/eval_jaxpr/ppermute | solution.py:15
  110.1 9.9 %collective-permute-start.1 = (f32[2,16,1,256]{3,2,1,0:T(1,128)S(1)}, f32[2,16,1,256]{3,2,1,0:T(1,128)S(1)}, u32[]{:S(2)}, u32[]{:S(2)}) collective-permute-start(f32[2,16,1,256]{3,2,1,0:T(1,128)S(1)} %pad_maximum_fusion.11), channel_id=1, source_target_pairs={{1,0},{2,1},{3,2},{4,3},{5,4},{6,5},{7,6},{9,8},{10,9},{11,10},{12... | collective-permute-start | bytes 98312 | tf_op jit(solution)/shard_map/while/body/eval_jaxpr/ppermute | solution.py:15
  111.4 8.5 %collective-permute-start = (f32[2,1,16,256]{3,2,1,0:T(8,128)S(1)}, f32[2,1,16,256]{3,2,1,0:T(8,128)S(1)}, u32[]{:S(2)}, u32[]{:S(2)}) collective-permute-start(f32[2,1,16,256]{3,2,1,0:T(8,128)S(1)} %pad_maximum_fusion.10), channel_id=1, source_target_pairs={{8,0},{16,8},{24,16},{9,1},{17,9},{25,17},{10,2},{18,10},{26,18},{... | collective-permute-start | bytes 98312 | tf_op jit(solution)/shard_map/while/body/eval_jaxpr/ppermute | solution.py:15
  123.0 12.4 %collective-permute-start.2 = (f32[2,16,1,256]{3,2,1,0:T(1,128)S(1)}, f32[2,16,1,256]{3,2,1,0:T(1,128)S(1)}, u32[]{:S(2)}, u32[]{:S(2)}) collective-permute-start(f32[2,16,1,256]{3,2,1,0:T(1,128)S(1)} %pad_maximum_fusion.12), channel_id=1, source_target_pairs={{0,1},{1,2},{2,3},{3,4},{4,5},{5,6},{6,7},{8,9},{9,10},{10,11},{11... | collective-permute-start | bytes 98312 | tf_op jit(solution)/shard_map/while/body/eval_jaxpr/ppermute | solution.py:15
  144.4 9.9 %collective-permute-start.1 = (f32[2,16,1,256]{3,2,1,0:T(1,128)S(1)}, f32[2,16,1,256]{3,2,1,0:T(1,128)S(1)}, u32[]{:S(2)}, u32[]{:S(2)}) collective-permute-start(f32[2,16,1,256]{3,2,1,0:T(1,128)S(1)} %pad_maximum_fusion.11), channel_id=1, source_target_pairs={{1,0},{2,1},{3,2},{4,3},{5,4},{6,5},{7,6},{9,8},{10,9},{11,10},{12... | collective-permute-start | bytes 98312 | tf_op jit(solution)/shard_map/while/body/eval_jaxpr/ppermute | solution.py:15
  145.7 8.5 %collective-permute-start = (f32[2,1,16,256]{3,2,1,0:T(8,128)S(1)}, f32[2,1,16,256]{3,2,1,0:T(8,128)S(1)}, u32[]{:S(2)}, u32[]{:S(2)}) collective-permute-start(f32[2,1,16,256]{3,2,1,0:T(8,128)S(1)} %pad_maximum_fusion.10), channel_id=1, source_target_pairs={{8,0},{16,8},{24,16},{9,1},{17,9},{25,17},{10,2},{18,10},{26,18},{... | collective-permute-start | bytes 98312 | tf_op jit(solution)/shard_map/while/body/eval_jaxpr/ppermute | solution.py:15
  157.3 12.4 %collective-permute-start.2 = (f32[2,16,1,256]{3,2,1,0:T(1,128)S(1)}, f32[2,16,1,256]{3,2,1,0:T(1,128)S(1)}, u32[]{:S(2)}, u32[]{:S(2)}) collective-permute-start(f32[2,16,1,256]{3,2,1,0:T(1,128)S(1)} %pad_maximum_fusion.12), channel_id=1, source_target_pairs={{0,1},{1,2},{2,3},{3,4},{4,5},{5,6},{6,7},{8,9},{9,10},{10,11},{11... | collective-permute-start | bytes 98312 | tf_op jit(solution)/shard_map/while/body/eval_jaxpr/ppermute | solution.py:15
  178.7 9.9 %collective-permute-start.1 = (f32[2,16,1,256]{3,2,1,0:T(1,128)S(1)}, f32[2,16,1,256]{3,2,1,0:T(1,128)S(1)}, u32[]{:S(2)}, u32[]{:S(2)}) collective-permute-start(f32[2,16,1,256]{3,2,1,0:T(1,128)S(1)} %pad_maximum_fusion.11), channel_id=1, source_target_pairs={{1,0},{2,1},{3,2},{4,3},{5,4},{6,5},{7,6},{9,8},{10,9},{11,10},{12... | collective-permute-start | bytes 98312 | tf_op jit(solution)/shard_map/while/body/eval_jaxpr/ppermute | solution.py:15
  180.0 8.5 %collective-permute-start = (f32[2,1,16,256]{3,2,1,0:T(8,128)S(1)}, f32[2,1,16,256]{3,2,1,0:T(8,128)S(1)}, u32[]{:S(2)}, u32[]{:S(2)}) collective-permute-start(f32[2,1,16,256]{3,2,1,0:T(8,128)S(1)} %pad_maximum_fusion.10), channel_id=1, source_target_pairs={{8,0},{16,8},{24,16},{9,1},{17,9},{25,17},{10,2},{18,10},{26,18},{... | collective-permute-start | bytes 98312 | tf_op jit(solution)/shard_map/while/body/eval_jaxpr/ppermute | solution.py:15
  191.6 12.4 %collective-permute-start.2 = (f32[2,16,1,256]{3,2,1,0:T(1,128)S(1)}, f32[2,16,1,256]{3,2,1,0:T(1,128)S(1)}, u32[]{:S(2)}, u32[]{:S(2)}) collective-permute-start(f32[2,16,1,256]{3,2,1,0:T(1,128)S(1)} %pad_maximum_fusion.12), channel_id=1, source_target_pairs={{0,1},{1,2},{2,3},{3,4},{4,5},{5,6},{6,7},{8,9},{9,10},{10,11},{11... | collective-permute-start | bytes 98312 | tf_op jit(solution)/shard_map/while/body/eval_jaxpr/ppermute | solution.py:15
  213.0 9.9 %collective-permute-start.1 = (f32[2,16,1,256]{3,2,1,0:T(1,128)S(1)}, f32[2,16,1,256]{3,2,1,0:T(1,128)S(1)}, u32[]{:S(2)}, u32[]{:S(2)}) collective-permute-start(f32[2,16,1,256]{3,2,1,0:T(1,128)S(1)} %pad_maximum_fusion.11), channel_id=1, source_target_pairs={{1,0},{2,1},{3,2},{4,3},{5,4},{6,5},{7,6},{9,8},{10,9},{11,10},{12... | collective-permute-start | bytes 98312 | tf_op jit(solution)/shard_map/while/body/eval_jaxpr/ppermute | solution.py:15
  214.3 8.5 %collective-permute-start = (f32[2,1,16,256]{3,2,1,0:T(8,128)S(1)}, f32[2,1,16,256]{3,2,1,0:T(8,128)S(1)}, u32[]{:S(2)}, u32[]{:S(2)}) collective-permute-start(f32[2,1,16,256]{3,2,1,0:T(8,128)S(1)} %pad_maximum_fusion.10), channel_id=1, source_target_pairs={{8,0},{16,8},{24,16},{9,1},{17,9},{25,17},{10,2},{18,10},{26,18},{... | collective-permute-start | bytes 98312 | tf_op jit(solution)/shard_map/while/body/eval_jaxpr/ppermute | solution.py:15
  225.9 12.4 %collective-permute-start.2 = (f32[2,16,1,256]{3,2,1,0:T(1,128)S(1)}, f32[2,16,1,256]{3,2,1,0:T(1,128)S(1)}, u32[]{:S(2)}, u32[]{:S(2)}) collective-permute-start(f32[2,16,1,256]{3,2,1,0:T(1,128)S(1)} %pad_maximum_fusion.12), channel_id=1, source_target_pairs={{0,1},{1,2},{2,3},{3,4},{4,5},{5,6},{6,7},{8,9},{9,10},{10,11},{11... | collective-permute-start | bytes 98312 | tf_op jit(solution)/shard_map/while/body/eval_jaxpr/ppermute | solution.py:15
  247.3 9.9 %collective-permute-start.1 = (f32[2,16,1,256]{3,2,1,0:T(1,128)S(1)}, f32[2,16,1,256]{3,2,1,0:T(1,128)S(1)}, u32[]{:S(2)}, u32[]{:S(2)}) collective-permute-start(f32[2,16,1,256]{3,2,1,0:T(1,128)S(1)} %pad_maximum_fusion.11), channel_id=1, source_target_pairs={{1,0},{2,1},{3,2},{4,3},{5,4},{6,5},{7,6},{9,8},{10,9},{11,10},{12... | collective-permute-start | bytes 98312 | tf_op jit(solution)/shard_map/while/body/eval_jaxpr/ppermute | solution.py:15
  248.6 8.5 %collective-permute-start = (f32[2,1,16,256]{3,2,1,0:T(8,128)S(1)}, f32[2,1,16,256]{3,2,1,0:T(8,128)S(1)}, u32[]{:S(2)}, u32[]{:S(2)}) collective-permute-start(f32[2,1,16,256]{3,2,1,0:T(8,128)S(1)} %pad_maximum_fusion.10), channel_id=1, source_target_pairs={{8,0},{16,8},{24,16},{9,1},{17,9},{25,17},{10,2},{18,10},{26,18},{... | collective-permute-start | bytes 98312 | tf_op jit(solution)/shard_map/while/body/eval_jaxpr/ppermute | solution.py:15
  260.2 12.4 %collective-permute-start.2 = (f32[2,16,1,256]{3,2,1,0:T(1,128)S(1)}, f32[2,16,1,256]{3,2,1,0:T(1,128)S(1)}, u32[]{:S(2)}, u32[]{:S(2)}) collective-permute-start(f32[2,16,1,256]{3,2,1,0:T(1,128)S(1)} %pad_maximum_fusion.12), channel_id=1, source_target_pairs={{0,1},{1,2},{2,3},{3,4},{4,5},{5,6},{6,7},{8,9},{9,10},{10,11},{11... | collective-permute-start | bytes 98312 | tf_op jit(solution)/shard_map/while/body/eval_jaxpr/ppermute | solution.py:15
  281.6 9.9 %collective-permute-start.1 = (f32[2,16,1,256]{3,2,1,0:T(1,128)S(1)}, f32[2,16,1,256]{3,2,1,0:T(1,128)S(1)}, u32[]{:S(2)}, u32[]{:S(2)}) collective-permute-start(f32[2,16,1,256]{3,2,1,0:T(1,128)S(1)} %pad_maximum_fusion.11), channel_id=1, source_target_pairs={{1,0},{2,1},{3,2},{4,3},{5,4},{6,5},{7,6},{9,8},{10,9},{11,10},{12... | collective-permute-start | bytes 98312 | tf_op jit(solution)/shard_map/while/body/eval_jaxpr/ppermute | solution.py:15
  282.9 8.5 %collective-permute-start = (f32[2,1,16,256]{3,2,1,0:T(8,128)S(1)}, f32[2,1,16,256]{3,2,1,0:T(8,128)S(1)}, u32[]{:S(2)}, u32[]{:S(2)}) collective-permute-start(f32[2,1,16,256]{3,2,1,0:T(8,128)S(1)} %pad_maximum_fusion.10), channel_id=1, source_target_pairs={{8,0},{16,8},{24,16},{9,1},{17,9},{25,17},{10,2},{18,10},{26,18},{... | collective-permute-start | bytes 98312 | tf_op jit(solution)/shard_map/while/body/eval_jaxpr/ppermute | solution.py:15
  294.5 12.4 %collective-permute-start.2 = (f32[2,16,1,256]{3,2,1,0:T(1,128)S(1)}, f32[2,16,1,256]{3,2,1,0:T(1,128)S(1)}, u32[]{:S(2)}, u32[]{:S(2)}) collective-permute-start(f32[2,16,1,256]{3,2,1,0:T(1,128)S(1)} %pad_maximum_fusion.12), channel_id=1, source_target_pairs={{0,1},{1,2},{2,3},{3,4},{4,5},{5,6},{6,7},{8,9},{9,10},{10,11},{11... | collective-permute-start | bytes 98312 | tf_op jit(solution)/shard_map/while/body/eval_jaxpr/ppermute | solution.py:15
  315.9 9.9 %collective-permute-start.1 = (f32[2,16,1,256]{3,2,1,0:T(1,128)S(1)}, f32[2,16,1,256]{3,2,1,0:T(1,128)S(1)}, u32[]{:S(2)}, u32[]{:S(2)}) collective-permute-start(f32[2,16,1,256]{3,2,1,0:T(1,128)S(1)} %pad_maximum_fusion.11), channel_id=1, source_target_pairs={{1,0},{2,1},{3,2},{4,3},{5,4},{6,5},{7,6},{9,8},{10,9},{11,10},{12... | collective-permute-start | bytes 98312 | tf_op jit(solution)/shard_map/while/body/eval_jaxpr/ppermute | solution.py:15
  317.2 8.5 %collective-permute-start = (f32[2,1,16,256]{3,2,1,0:T(8,128)S(1)}, f32[2,1,16,256]{3,2,1,0:T(8,128)S(1)}, u32[]{:S(2)}, u32[]{:S(2)}) collective-permute-start(f32[2,1,16,256]{3,2,1,0:T(8,128)S(1)} %pad_maximum_fusion.10), channel_id=1, source_target_pairs={{8,0},{16,8},{24,16},{9,1},{17,9},{25,17},{10,2},{18,10},{26,18},{... | collective-permute-start | bytes 98312 | tf_op jit(solution)/shard_map/while/body/eval_jaxpr/ppermute | solution.py:15
  328.8 12.4 %collective-permute-start.2 = (f32[2,16,1,256]{3,2,1,0:T(1,128)S(1)}, f32[2,16,1,256]{3,2,1,0:T(1,128)S(1)}, u32[]{:S(2)}, u32[]{:S(2)}) collective-permute-start(f32[2,16,1,256]{3,2,1,0:T(1,128)S(1)} %pad_maximum_fusion.12), channel_id=1, source_target_pairs={{0,1},{1,2},{2,3},{3,4},{4,5},{5,6},{6,7},{8,9},{9,10},{10,11},{11... | collective-permute-start | bytes 98312 | tf_op jit(solution)/shard_map/while/body/eval_jaxpr/ppermute | solution.py:15
  350.2 9.9 %collective-permute-start.1 = (f32[2,16,1,256]{3,2,1,0:T(1,128)S(1)}, f32[2,16,1,256]{3,2,1,0:T(1,128)S(1)}, u32[]{:S(2)}, u32[]{:S(2)}) collective-permute-start(f32[2,16,1,256]{3,2,1,0:T(1,128)S(1)} %pad_maximum_fusion.11), channel_id=1, source_target_pairs={{1,0},{2,1},{3,2},{4,3},{5,4},{6,5},{7,6},{9,8},{10,9},{11,10},{12... | collective-permute-start | bytes 98312 | tf_op jit(solution)/shard_map/while/body/eval_jaxpr/ppermute | solution.py:15
  351.5 8.5 %collective-permute-start = (f32[2,1,16,256]{3,2,1,0:T(8,128)S(1)}, f32[2,1,16,256]{3,2,1,0:T(8,128)S(1)}, u32[]{:S(2)}, u32[]{:S(2)}) collective-permute-start(f32[2,1,16,256]{3,2,1,0:T(8,128)S(1)} %pad_maximum_fusion.10), channel_id=1, source_target_pairs={{8,0},{16,8},{24,16},{9,1},{17,9},{25,17},{10,2},{18,10},{26,18},{... | collective-permute-start | bytes 98312 | tf_op jit(solution)/shard_map/while/body/eval_jaxpr/ppermute | solution.py:15
  363.1 12.4 %collective-permute-start.2 = (f32[2,16,1,256]{3,2,1,0:T(1,128)S(1)}, f32[2,16,1,256]{3,2,1,0:T(1,128)S(1)}, u32[]{:S(2)}, u32[]{:S(2)}) collective-permute-start(f32[2,16,1,256]{3,2,1,0:T(1,128)S(1)} %pad_maximum_fusion.12), channel_id=1, source_target_pairs={{0,1},{1,2},{2,3},{3,4},{4,5},{5,6},{6,7},{8,9},{9,10},{10,11},{11... | collective-permute-start | bytes 98312 | tf_op jit(solution)/shard_map/while/body/eval_jaxpr/ppermute | solution.py:15
  384.5 9.9 %collective-permute-start.1 = (f32[2,16,1,256]{3,2,1,0:T(1,128)S(1)}, f32[2,16,1,256]{3,2,1,0:T(1,128)S(1)}, u32[]{:S(2)}, u32[]{:S(2)}) collective-permute-start(f32[2,16,1,256]{3,2,1,0:T(1,128)S(1)} %pad_maximum_fusion.11), channel_id=1, source_target_pairs={{1,0},{2,1},{3,2},{4,3},{5,4},{6,5},{7,6},{9,8},{10,9},{11,10},{12... | collective-permute-start | bytes 98312 | tf_op jit(solution)/shard_map/while/body/eval_jaxpr/ppermute | solution.py:15
  385.8 8.5 %collective-permute-start = (f32[2,1,16,256]{3,2,1,0:T(8,128)S(1)}, f32[2,1,16,256]{3,2,1,0:T(8,128)S(1)}, u32[]{:S(2)}, u32[]{:S(2)}) collective-permute-start(f32[2,1,16,256]{3,2,1,0:T(8,128)S(1)} %pad_maximum_fusion.10), channel_id=1, source_target_pairs={{8,0},{16,8},{24,16},{9,1},{17,9},{25,17},{10,2},{18,10},{26,18},{... | collective-permute-start | bytes 98312 | tf_op jit(solution)/shard_map/while/body/eval_jaxpr/ppermute | solution.py:15
  397.4 12.4 %collective-permute-start.2 = (f32[2,16,1,256]{3,2,1,0:T(1,128)S(1)}, f32[2,16,1,256]{3,2,1,0:T(1,128)S(1)}, u32[]{:S(2)}, u32[]{:S(2)}) collective-permute-start(f32[2,16,1,256]{3,2,1,0:T(1,128)S(1)} %pad_maximum_fusion.12), channel_id=1, source_target_pairs={{0,1},{1,2},{2,3},{3,4},{4,5},{5,6},{6,7},{8,9},{9,10},{10,11},{11... | collective-permute-start | bytes 98312 | tf_op jit(solution)/shard_map/while/body/eval_jaxpr/ppermute | solution.py:15
  418.8 9.9 %collective-permute-start.1 = (f32[2,16,1,256]{3,2,1,0:T(1,128)S(1)}, f32[2,16,1,256]{3,2,1,0:T(1,128)S(1)}, u32[]{:S(2)}, u32[]{:S(2)}) collective-permute-start(f32[2,16,1,256]{3,2,1,0:T(1,128)S(1)} %pad_maximum_fusion.11), channel_id=1, source_target_pairs={{1,0},{2,1},{3,2},{4,3},{5,4},{6,5},{7,6},{9,8},{10,9},{11,10},{12... | collective-permute-start | bytes 98312 | tf_op jit(solution)/shard_map/while/body/eval_jaxpr/ppermute | solution.py:15
  420.1 8.5 %collective-permute-start = (f32[2,1,16,256]{3,2,1,0:T(8,128)S(1)}, f32[2,1,16,256]{3,2,1,0:T(8,128)S(1)}, u32[]{:S(2)}, u32[]{:S(2)}) collective-permute-start(f32[2,1,16,256]{3,2,1,0:T(8,128)S(1)} %pad_maximum_fusion.10), channel_id=1, source_target_pairs={{8,0},{16,8},{24,16},{9,1},{17,9},{25,17},{10,2},{18,10},{26,18},{... | collective-permute-start | bytes 98312 | tf_op jit(solution)/shard_map/while/body/eval_jaxpr/ppermute | solution.py:15
  431.7 12.4 %collective-permute-start.2 = (f32[2,16,1,256]{3,2,1,0:T(1,128)S(1)}, f32[2,16,1,256]{3,2,1,0:T(1,128)S(1)}, u32[]{:S(2)}, u32[]{:S(2)}) collective-permute-start(f32[2,16,1,256]{3,2,1,0:T(1,128)S(1)} %pad_maximum_fusion.12), channel_id=1, source_target_pairs={{0,1},{1,2},{2,3},{3,4},{4,5},{5,6},{6,7},{8,9},{9,10},{10,11},{11... | collective-permute-start | bytes 98312 | tf_op jit(solution)/shard_map/while/body/eval_jaxpr/ppermute | solution.py:15
  453.1 9.9 %collective-permute-start.1 = (f32[2,16,1,256]{3,2,1,0:T(1,128)S(1)}, f32[2,16,1,256]{3,2,1,0:T(1,128)S(1)}, u32[]{:S(2)}, u32[]{:S(2)}) collective-permute-start(f32[2,16,1,256]{3,2,1,0:T(1,128)S(1)} %pad_maximum_fusion.11), channel_id=1, source_target_pairs={{1,0},{2,1},{3,2},{4,3},{5,4},{6,5},{7,6},{9,8},{10,9},{11,10},{12... | collective-permute-start | bytes 98312 | tf_op jit(solution)/shard_map/while/body/eval_jaxpr/ppermute | solution.py:15
  454.4 8.5 %collective-permute-start = (f32[2,1,16,256]{3,2,1,0:T(8,128)S(1)}, f32[2,1,16,256]{3,2,1,0:T(8,128)S(1)}, u32[]{:S(2)}, u32[]{:S(2)}) collective-permute-start(f32[2,1,16,256]{3,2,1,0:T(8,128)S(1)} %pad_maximum_fusion.10), channel_id=1, source_target_pairs={{8,0},{16,8},{24,16},{9,1},{17,9},{25,17},{10,2},{18,10},{26,18},{... | collective-permute-start | bytes 98312 | tf_op jit(solution)/shard_map/while/body/eval_jaxpr/ppermute | solution.py:15
  466.0 12.4 %collective-permute-start.2 = (f32[2,16,1,256]{3,2,1,0:T(1,128)S(1)}, f32[2,16,1,256]{3,2,1,0:T(1,128)S(1)}, u32[]{:S(2)}, u32[]{:S(2)}) collective-permute-start(f32[2,16,1,256]{3,2,1,0:T(1,128)S(1)} %pad_maximum_fusion.12), channel_id=1, source_target_pairs={{0,1},{1,2},{2,3},{3,4},{4,5},{5,6},{6,7},{8,9},{9,10},{10,11},{11... | collective-permute-start | bytes 98312 | tf_op jit(solution)/shard_map/while/body/eval_jaxpr/ppermute | solution.py:15
  487.4 9.9 %collective-permute-start.1 = (f32[2,16,1,256]{3,2,1,0:T(1,128)S(1)}, f32[2,16,1,256]{3,2,1,0:T(1,128)S(1)}, u32[]{:S(2)}, u32[]{:S(2)}) collective-permute-start(f32[2,16,1,256]{3,2,1,0:T(1,128)S(1)} %pad_maximum_fusion.11), channel_id=1, source_target_pairs={{1,0},{2,1},{3,2},{4,3},{5,4},{6,5},{7,6},{9,8},{10,9},{11,10},{12... | collective-permute-start | bytes 98312 | tf_op jit(solution)/shard_map/while/body/eval_jaxpr/ppermute | solution.py:15
  488.7 8.5 %collective-permute-start = (f32[2,1,16,256]{3,2,1,0:T(8,128)S(1)}, f32[2,1,16,256]{3,2,1,0:T(8,128)S(1)}, u32[]{:S(2)}, u32[]{:S(2)}) collective-permute-start(f32[2,1,16,256]{3,2,1,0:T(8,128)S(1)} %pad_maximum_fusion.10), channel_id=1, source_target_pairs={{8,0},{16,8},{24,16},{9,1},{17,9},{25,17},{10,2},{18,10},{26,18},{... | collective-permute-start | bytes 98312 | tf_op jit(solution)/shard_map/while/body/eval_jaxpr/ppermute | solution.py:15
  500.3 12.4 %collective-permute-start.2 = (f32[2,16,1,256]{3,2,1,0:T(1,128)S(1)}, f32[2,16,1,256]{3,2,1,0:T(1,128)S(1)}, u32[]{:S(2)}, u32[]{:S(2)}) collective-permute-start(f32[2,16,1,256]{3,2,1,0:T(1,128)S(1)} %pad_maximum_fusion.12), channel_id=1, source_target_pairs={{0,1},{1,2},{2,3},{3,4},{4,5},{5,6},{6,7},{8,9},{9,10},{10,11},{11... | collective-permute-start | bytes 98312 | tf_op jit(solution)/shard_map/while/body/eval_jaxpr/ppermute | solution.py:15
  521.7 9.9 %collective-permute-start.1 = (f32[2,16,1,256]{3,2,1,0:T(1,128)S(1)}, f32[2,16,1,256]{3,2,1,0:T(1,128)S(1)}, u32[]{:S(2)}, u32[]{:S(2)}) collective-permute-start(f32[2,16,1,256]{3,2,1,0:T(1,128)S(1)} %pad_maximum_fusion.11), channel_id=1, source_target_pairs={{1,0},{2,1},{3,2},{4,3},{5,4},{6,5},{7,6},{9,8},{10,9},{11,10},{12... | collective-permute-start | bytes 98312 | tf_op jit(solution)/shard_map/while/body/eval_jaxpr/ppermute | solution.py:15
  523.0 8.5 %collective-permute-start = (f32[2,1,16,256]{3,2,1,0:T(8,128)S(1)}, f32[2,1,16,256]{3,2,1,0:T(8,128)S(1)}, u32[]{:S(2)}, u32[]{:S(2)}) collective-permute-start(f32[2,1,16,256]{3,2,1,0:T(8,128)S(1)} %pad_maximum_fusion.10), channel_id=1, source_target_pairs={{8,0},{16,8},{24,16},{9,1},{17,9},{25,17},{10,2},{18,10},{26,18},{... | collective-permute-start | bytes 98312 | tf_op jit(solution)/shard_map/while/body/eval_jaxpr/ppermute | solution.py:15
  534.6 12.4 %collective-permute-start.2 = (f32[2,16,1,256]{3,2,1,0:T(1,128)S(1)}, f32[2,16,1,256]{3,2,1,0:T(1,128)S(1)}, u32[]{:S(2)}, u32[]{:S(2)}) collective-permute-start(f32[2,16,1,256]{3,2,1,0:T(1,128)S(1)} %pad_maximum_fusion.12), channel_id=1, source_target_pairs={{0,1},{1,2},{2,3},{3,4},{4,5},{5,6},{6,7},{8,9},{9,10},{10,11},{11... | collective-permute-start | bytes 98312 | tf_op jit(solution)/shard_map/while/body/eval_jaxpr/ppermute | solution.py:15
  (440 other events, 2458.9 us)
where the time goes:
time: 612 us; the launch traced here: 605 us
  starting transfers between devices  205 us (33%)
  local copies, waits for them, and re-layouts  160 us (26%)
  other arithmetic  119 us (19%)
  matrix products  52.2 us (9%)
  blocking collectives  45.9 us (8%)
  waiting for transfers between devices  13.2 us (2%)
  loops' own time  7.44 us (1%)
    ppermute x64, starting transfers between devices, passed_along(): return lax.ppermute(block, axis, route)  205 us
    slice x96, local copies, waits for them, and re-layouts, difference(): lax.slice_in_dim(values, 1, length, axis=axis)  73.3 us
    sub x48, other arithmetic, turn_parts(): field_h[number] - courant * rotation[number]  50.2 us
    psum x1, blocking collectives, local(): port_power = lax.psum(partial_value, ('gx', 'gy'))  45.9 us
    add x16, other arithmetic, turn_parts(): field_e[1] + factor * rotation[1]  38.7 us
    while x832, local copies, waits for them, and re-layouts  36.9 us
    dot_general x16, matrix products, inject(): lax.dot_general(weighted, depth_table, (((0,), (0,)), ((), ())), precisio...  30.5 us
    dynamic_update_slice x16, local copies, waits for them, and re-layouts, note_power(): return lax.dynamic_update_slice_in_dim(record, drive[None, :], index, 0)  21.4 us
  transfers between devices with their start and end apart: 64, of which 16 were waited for; matrix products, arithmetic and copies ran while one was open for 22% of the time, Pallas kernels for 0%

commit v1 on v0

--- a/solution.py
+++ b/solution.py
@@ -134,7 +134,7 @@
     electric = jnp.stack(parts_e)
     magnetic = jnp.stack(parts_h)
     partial_value = jnp.dot(record, members, precision=lax.Precision.HIGHEST)
-    port_power = lax.psum(partial_value, ("gx", "gy"))
+    port_power = jnp.sum(lax.all_gather(partial_value, ("gx", "gy")), axis=0)
     return (electric, magnetic, port_power)
 
 

time: 612 us -> 637 us (1.041)
  waiting for transfers between devices: 13.2 us -> 70.3 us
  blocking collectives: 45.9 us -> 0 us
  between operations: 1.44 us -> 14.9 us
    all_gather x0 -> x1, waiting for transfers between devices: none -> 57.1 us  [local(): port_power = jnp.sum(lax.all_gather(partial_value, ('gx', 'gy')), axis=0)]
    psum x1 -> x0, blocking collectives: 45.9 us -> none  [local(): port_power = lax.psum(partial_value, ('gx', 'gy'))]
  transfers between devices with their start and end apart: 64 -> 65, of which waited for: 16 -> 17; matrix products, arithmetic and copies ran while one was open for 22% -> 21% of each run, Pallas kernels for 0% -> 0%
where the time goes in v1:
time: 637 us; the launch traced here: 630 us
  starting transfers between devices  205 us (32%)
  local copies, waits for them, and re-layouts  160 us (25%)
  other arithmetic  121 us (19%)
  waiting for transfers between devices  70.3 us (11%)
  matrix products  51.7 us (8%)
  between operations  14.9 us (2%)
  loops' own time  7.45 us (1%)
    ppermute x64, starting transfers between devices, passed_along(): return lax.ppermute(block, axis, route)  205 us
    slice x96, local copies, waits for them, and re-layouts, difference(): lax.slice_in_dim(values, 1, length, axis=axis)  73.4 us
    all_gather x1, waiting for transfers between devices, local(): port_power = jnp.sum(lax.all_gather(partial_value, ('gx', 'gy')), axis=0)  57.1 us
    sub x48, other arithmetic, turn_parts(): field_h[number] - courant * rotation[number]  50.3 us
    add x16, other arithmetic, turn_parts(): field_e[1] + factor * rotation[1]  38.4 us
    while x832, local copies, waits for them, and re-layouts  36.6 us
    dot_general x16, matrix products, inject(): lax.dot_general(weighted, depth_table, (((0,), (0,)), ((), ())), precisio...  30.1 us
    dynamic_update_slice x16, local copies, waits for them, and re-layouts, note_power(): return lax.dynamic_update_slice_in_dim(record, drive[None, :], index, 0)  21.4 us
  transfers between devices with their start and end apart: 65, of which 17 were waited for; matrix products, arithmetic and copies ran while one was open for 21% of the time, Pallas kernels for 0%

profile of v1, /device:TPU:0, one launch (start us, length us, event | category | flops | bytes accessed | tf_op | source)
XLA Modules:
  0.0 630.5 jit_solution(7696495321807315751)
XLA Ops:
  16.2 544.6 %while.50 = (s32[]{:T(128)}, f32[16,16,256]{2,1,0:T(8,128)S(1)}, f32[16,16,256]{2,1,0:T(8,128)S(1)}, f32[16,16,256]{2,1,0:T(8,128)S(1)}, f32[16,16,256]{2,1,0:T(...) while((s32[]{:T(128)}, f32[16,16,256]{2,1,0:T(8,128)S(1)}, ...), condition=%wide.region_2.3_spmd.clone, body=%wide.region_0.2_spmd.clone.sunk | while | flops 812285952 | bytes 56044672 | solution.py:133
  26.2 2.4 multiply_subtract_fusion.7
  29.2 5.5 collective-permute-start.2
  36.6 2.8 collective-permute-start.3
  58.2 2.4 multiply_subtract_fusion.7
  61.2 5.4 collective-permute-start.2
  68.6 3.8 collective-permute-start.3
  91.3 2.4 multiply_subtract_fusion.7
  94.3 5.2 collective-permute-start.2
  101.3 5.3 collective-permute-start.3
  125.5 2.4 multiply_subtract_fusion.7
  128.5 5.2 collective-permute-start.2
  135.6 5.3 collective-permute-start.3
  159.8 2.4 multiply_subtract_fusion.7
  162.8 5.2 collective-permute-start.2
  169.8 5.3 collective-permute-start.3
  194.0 2.4 multiply_subtract_fusion.7
  197.0 5.2 collective-permute-start.2
  204.1 5.3 collective-permute-start.3
  231.3 5.2 collective-permute-start.2
  238.3 5.3 collective-permute-start.3
  262.5 2.4 multiply_subtract_fusion.7
  265.5 5.2 collective-permute-start.2
  272.6 5.3 collective-permute-start.3
  296.8 2.4 multiply_subtract_fusion.7
  299.8 5.2 collective-permute-start.2
  306.8 5.3 collective-permute-start.3
  331.0 2.4 multiply_subtract_fusion.7
  334.0 5.2 collective-permute-start.2
  341.1 5.3 collective-permute-start.3
  365.3 2.4 multiply_subtract_fusion.7
  368.3 5.2 collective-permute-start.2
  375.3 5.3 collective-permute-start.3
  399.5 2.4 multiply_subtract_fusion.7
  402.5 5.2 collective-permute-start.2
  409.6 5.3 collective-permute-start.3
  433.8 2.4 multiply_subtract_fusion.7
  436.8 5.2 collective-permute-start.2
  443.8 5.3 collective-permute-start.3
  468.0 2.4 multiply_subtract_fusion.7
  471.0 5.2 collective-permute-start.2
  478.1 5.3 collective-permute-start.3
  502.3 2.4 multiply_subtract_fusion.7
  505.3 5.2 collective-permute-start.2
  512.3 5.3 collective-permute-start.3
  539.5 5.2 collective-permute-start.2
  546.6 5.3 collective-permute-start.3
  564.6 57.1 %all-gather.3.cloned.1.call-done = f32[512,512]{1,0:T(8,128)} async-done(((f32[16,512]{1,0:T(8,128)}), f32[512,512]{1,0:T(8,128)}) %all-gather.3.cloned.1.call-update) | async-done | bytes 1048592 | tf_op jit(solution)/shard_map/all_gather | solution.py:137
  (1475 shorter events, 352.8 us)
Async XLA Ops:
  7.2 614.5 %all-gather.3.cloned.1.call-start = ((), (), s32[]{:S(2)}) async-start(), calls=%async_computation | async-start | bytes 1081344 | tf_op jit(solution)/shard_map/all_gather | solution.py:137
  16.3 9.8 %collective-permute-start.1 = (f32[2,16,1,256]{3,2,1,0:T(1,128)S(1)}, f32[2,16,1,256]{3,2,1,0:T(1,128)S(1)}, u32[]{:S(2)}, u32[]{:S(2)}) collective-permute-start(f32[2,16,1,256]{3,2,1,0:T(1,128)S(1)} %pad_maximum_fusion.11), channel_id=1, source_target_pairs={{1,0},{2,1},{3,2},{4,3},{5,4},{6,5},{7,6},{9,8},{10,9},{11,10},{12... | collective-permute-start | bytes 98312 | tf_op jit(solution)/shard_map/while/body/eval_jaxpr/ppermute | solution.py:15
  17.6 8.5 %collective-permute-start = (f32[2,1,16,256]{3,2,1,0:T(8,128)S(1)}, f32[2,1,16,256]{3,2,1,0:T(8,128)S(1)}, u32[]{:S(2)}, u32[]{:S(2)}) collective-permute-start(f32[2,1,16,256]{3,2,1,0:T(8,128)S(1)} %pad_maximum_fusion.10), channel_id=1, source_target_pairs={{8,0},{16,8},{24,16},{9,1},{17,9},{25,17},{10,2},{18,10},{26,18},{... | collective-permute-start | bytes 98312 | tf_op jit(solution)/shard_map/while/body/eval_jaxpr/ppermute | solution.py:15
  29.2 10.2 %collective-permute-start.2 = (f32[2,16,1,256]{3,2,1,0:T(1,128)S(1)}, f32[2,16,1,256]{3,2,1,0:T(1,128)S(1)}, u32[]{:S(2)}, u32[]{:S(2)}) collective-permute-start(f32[2,16,1,256]{3,2,1,0:T(1,128)S(1)} %pad_maximum_fusion.12), channel_id=1, source_target_pairs={{0,1},{1,2},{2,3},{3,4},{4,5},{5,6},{6,7},{8,9},{9,10},{10,11},{11... | collective-permute-start | bytes 98312 | tf_op jit(solution)/shard_map/while/body/eval_jaxpr/ppermute | solution.py:15
  48.3 9.8 %collective-permute-start.1 = (f32[2,16,1,256]{3,2,1,0:T(1,128)S(1)}, f32[2,16,1,256]{3,2,1,0:T(1,128)S(1)}, u32[]{:S(2)}, u32[]{:S(2)}) collective-permute-start(f32[2,16,1,256]{3,2,1,0:T(1,128)S(1)} %pad_maximum_fusion.11), channel_id=1, source_target_pairs={{1,0},{2,1},{3,2},{4,3},{5,4},{6,5},{7,6},{9,8},{10,9},{11,10},{12... | collective-permute-start | bytes 98312 | tf_op jit(solution)/shard_map/while/body/eval_jaxpr/ppermute | solution.py:15
  49.7 8.5 %collective-permute-start = (f32[2,1,16,256]{3,2,1,0:T(8,128)S(1)}, f32[2,1,16,256]{3,2,1,0:T(8,128)S(1)}, u32[]{:S(2)}, u32[]{:S(2)}) collective-permute-start(f32[2,1,16,256]{3,2,1,0:T(8,128)S(1)} %pad_maximum_fusion.10), channel_id=1, source_target_pairs={{8,0},{16,8},{24,16},{9,1},{17,9},{25,17},{10,2},{18,10},{26,18},{... | collective-permute-start | bytes 98312 | tf_op jit(solution)/shard_map/while/body/eval_jaxpr/ppermute | solution.py:15
  61.2 11.2 %collective-permute-start.2 = (f32[2,16,1,256]{3,2,1,0:T(1,128)S(1)}, f32[2,16,1,256]{3,2,1,0:T(1,128)S(1)}, u32[]{:S(2)}, u32[]{:S(2)}) collective-permute-start(f32[2,16,1,256]{3,2,1,0:T(1,128)S(1)} %pad_maximum_fusion.12), channel_id=1, source_target_pairs={{0,1},{1,2},{2,3},{3,4},{4,5},{5,6},{6,7},{8,9},{9,10},{10,11},{11... | collective-permute-start | bytes 98312 | tf_op jit(solution)/shard_map/while/body/eval_jaxpr/ppermute | solution.py:15
  81.4 9.8 %collective-permute-start.1 = (f32[2,16,1,256]{3,2,1,0:T(1,128)S(1)}, f32[2,16,1,256]{3,2,1,0:T(1,128)S(1)}, u32[]{:S(2)}, u32[]{:S(2)}) collective-permute-start(f32[2,16,1,256]{3,2,1,0:T(1,128)S(1)} %pad_maximum_fusion.11), channel_id=1, source_target_pairs={{1,0},{2,1},{3,2},{4,3},{5,4},{6,5},{7,6},{9,8},{10,9},{11,10},{12... | collective-permute-start | bytes 98312 | tf_op jit(solution)/shard_map/while/body/eval_jaxpr/ppermute | solution.py:15
  82.7 8.5 %collective-permute-start = (f32[2,1,16,256]{3,2,1,0:T(8,128)S(1)}, f32[2,1,16,256]{3,2,1,0:T(8,128)S(1)}, u32[]{:S(2)}, u32[]{:S(2)}) collective-permute-start(f32[2,1,16,256]{3,2,1,0:T(8,128)S(1)} %pad_maximum_fusion.10), channel_id=1, source_target_pairs={{8,0},{16,8},{24,16},{9,1},{17,9},{25,17},{10,2},{18,10},{26,18},{... | collective-permute-start | bytes 98312 | tf_op jit(solution)/shard_map/while/body/eval_jaxpr/ppermute | solution.py:15
  94.3 12.4 %collective-permute-start.2 = (f32[2,16,1,256]{3,2,1,0:T(1,128)S(1)}, f32[2,16,1,256]{3,2,1,0:T(1,128)S(1)}, u32[]{:S(2)}, u32[]{:S(2)}) collective-permute-start(f32[2,16,1,256]{3,2,1,0:T(1,128)S(1)} %pad_maximum_fusion.12), channel_id=1, source_target_pairs={{0,1},{1,2},{2,3},{3,4},{4,5},{5,6},{6,7},{8,9},{9,10},{10,11},{11... | collective-permute-start | bytes 98312 | tf_op jit(solution)/shard_map/while/body/eval_jaxpr/ppermute | solution.py:15
  115.6 9.8 %collective-permute-start.1 = (f32[2,16,1,256]{3,2,1,0:T(1,128)S(1)}, f32[2,16,1,256]{3,2,1,0:T(1,128)S(1)}, u32[]{:S(2)}, u32[]{:S(2)}) collective-permute-start(f32[2,16,1,256]{3,2,1,0:T(1,128)S(1)} %pad_maximum_fusion.11), channel_id=1, source_target_pairs={{1,0},{2,1},{3,2},{4,3},{5,4},{6,5},{7,6},{9,8},{10,9},{11,10},{12... | collective-permute-start | bytes 98312 | tf_op jit(solution)/shard_map/while/body/eval_jaxpr/ppermute | solution.py:15
  117.0 8.5 %collective-permute-start = (f32[2,1,16,256]{3,2,1,0:T(8,128)S(1)}, f32[2,1,16,256]{3,2,1,0:T(8,128)S(1)}, u32[]{:S(2)}, u32[]{:S(2)}) collective-permute-start(f32[2,1,16,256]{3,2,1,0:T(8,128)S(1)} %pad_maximum_fusion.10), channel_id=1, source_target_pairs={{8,0},{16,8},{24,16},{9,1},{17,9},{25,17},{10,2},{18,10},{26,18},{... | collective-permute-start | bytes 98312 | tf_op jit(solution)/shard_map/while/body/eval_jaxpr/ppermute | solution.py:15
  128.5 12.4 %collective-permute-start.2 = (f32[2,16,1,256]{3,2,1,0:T(1,128)S(1)}, f32[2,16,1,256]{3,2,1,0:T(1,128)S(1)}, u32[]{:S(2)}, u32[]{:S(2)}) collective-permute-start(f32[2,16,1,256]{3,2,1,0:T(1,128)S(1)} %pad_maximum_fusion.12), channel_id=1, source_target_pairs={{0,1},{1,2},{2,3},{3,4},{4,5},{5,6},{6,7},{8,9},{9,10},{10,11},{11... | collective-permute-start | bytes 98312 | tf_op jit(solution)/shard_map/while/body/eval_jaxpr/ppermute | solution.py:15
  149.9 9.8 %collective-permute-start.1 = (f32[2,16,1,256]{3,2,1,0:T(1,128)S(1)}, f32[2,16,1,256]{3,2,1,0:T(1,128)S(1)}, u32[]{:S(2)}, u32[]{:S(2)}) collective-permute-start(f32[2,16,1,256]{3,2,1,0:T(1,128)S(1)} %pad_maximum_fusion.11), channel_id=1, source_target_pairs={{1,0},{2,1},{3,2},{4,3},{5,4},{6,5},{7,6},{9,8},{10,9},{11,10},{12... | collective-permute-start | bytes 98312 | tf_op jit(solution)/shard_map/while/body/eval_jaxpr/ppermute | solution.py:15
  151.2 8.5 %collective-permute-start = (f32[2,1,16,256]{3,2,1,0:T(8,128)S(1)}, f32[2,1,16,256]{3,2,1,0:T(8,128)S(1)}, u32[]{:S(2)}, u32[]{:S(2)}) collective-permute-start(f32[2,1,16,256]{3,2,1,0:T(8,128)S(1)} %pad_maximum_fusion.10), channel_id=1, source_target_pairs={{8,0},{16,8},{24,16},{9,1},{17,9},{25,17},{10,2},{18,10},{26,18},{... | collective-permute-start | bytes 98312 | tf_op jit(solution)/shard_map/while/body/eval_jaxpr/ppermute | solution.py:15
  162.8 12.4 %collective-permute-start.2 = (f32[2,16,1,256]{3,2,1,0:T(1,128)S(1)}, f32[2,16,1,256]{3,2,1,0:T(1,128)S(1)}, u32[]{:S(2)}, u32[]{:S(2)}) collective-permute-start(f32[2,16,1,256]{3,2,1,0:T(1,128)S(1)} %pad_maximum_fusion.12), channel_id=1, source_target_pairs={{0,1},{1,2},{2,3},{3,4},{4,5},{5,6},{6,7},{8,9},{9,10},{10,11},{11... | collective-permute-start | bytes 98312 | tf_op jit(solution)/shard_map/while/body/eval_jaxpr/ppermute | solution.py:15
  184.1 9.8 %collective-permute-start.1 = (f32[2,16,1,256]{3,2,1,0:T(1,128)S(1)}, f32[2,16,1,256]{3,2,1,0:T(1,128)S(1)}, u32[]{:S(2)}, u32[]{:S(2)}) collective-permute-start(f32[2,16,1,256]{3,2,1,0:T(1,128)S(1)} %pad_maximum_fusion.11), channel_id=1, source_target_pairs={{1,0},{2,1},{3,2},{4,3},{5,4},{6,5},{7,6},{9,8},{10,9},{11,10},{12... | collective-permute-start | bytes 98312 | tf_op jit(solution)/shard_map/while/body/eval_jaxpr/ppermute | solution.py:15
  185.5 8.5 %collective-permute-start = (f32[2,1,16,256]{3,2,1,0:T(8,128)S(1)}, f32[2,1,16,256]{3,2,1,0:T(8,128)S(1)}, u32[]{:S(2)}, u32[]{:S(2)}) collective-permute-start(f32[2,1,16,256]{3,2,1,0:T(8,128)S(1)} %pad_maximum_fusion.10), channel_id=1, source_target_pairs={{8,0},{16,8},{24,16},{9,1},{17,9},{25,17},{10,2},{18,10},{26,18},{... | collective-permute-start | bytes 98312 | tf_op jit(solution)/shard_map/while/body/eval_jaxpr/ppermute | solution.py:15
  197.0 12.4 %collective-permute-start.2 = (f32[2,16,1,256]{3,2,1,0:T(1,128)S(1)}, f32[2,16,1,256]{3,2,1,0:T(1,128)S(1)}, u32[]{:S(2)}, u32[]{:S(2)}) collective-permute-start(f32[2,16,1,256]{3,2,1,0:T(1,128)S(1)} %pad_maximum_fusion.12), channel_id=1, source_target_pairs={{0,1},{1,2},{2,3},{3,4},{4,5},{5,6},{6,7},{8,9},{9,10},{10,11},{11... | collective-permute-start | bytes 98312 | tf_op jit(solution)/shard_map/while/body/eval_jaxpr/ppermute | solution.py:15
  218.4 9.8 %collective-permute-start.1 = (f32[2,16,1,256]{3,2,1,0:T(1,128)S(1)}, f32[2,16,1,256]{3,2,1,0:T(1,128)S(1)}, u32[]{:S(2)}, u32[]{:S(2)}) collective-permute-start(f32[2,16,1,256]{3,2,1,0:T(1,128)S(1)} %pad_maximum_fusion.11), channel_id=1, source_target_pairs={{1,0},{2,1},{3,2},{4,3},{5,4},{6,5},{7,6},{9,8},{10,9},{11,10},{12... | collective-permute-start | bytes 98312 | tf_op jit(solution)/shard_map/while/body/eval_jaxpr/ppermute | solution.py:15
  219.7 8.5 %collective-permute-start = (f32[2,1,16,256]{3,2,1,0:T(8,128)S(1)}, f32[2,1,16,256]{3,2,1,0:T(8,128)S(1)}, u32[]{:S(2)}, u32[]{:S(2)}) collective-permute-start(f32[2,1,16,256]{3,2,1,0:T(8,128)S(1)} %pad_maximum_fusion.10), channel_id=1, source_target_pairs={{8,0},{16,8},{24,16},{9,1},{17,9},{25,17},{10,2},{18,10},{26,18},{... | collective-permute-start | bytes 98312 | tf_op jit(solution)/shard_map/while/body/eval_jaxpr/ppermute | solution.py:15
  231.3 12.4 %collective-permute-start.2 = (f32[2,16,1,256]{3,2,1,0:T(1,128)S(1)}, f32[2,16,1,256]{3,2,1,0:T(1,128)S(1)}, u32[]{:S(2)}, u32[]{:S(2)}) collective-permute-start(f32[2,16,1,256]{3,2,1,0:T(1,128)S(1)} %pad_maximum_fusion.12), channel_id=1, source_target_pairs={{0,1},{1,2},{2,3},{3,4},{4,5},{5,6},{6,7},{8,9},{9,10},{10,11},{11... | collective-permute-start | bytes 98312 | tf_op jit(solution)/shard_map/while/body/eval_jaxpr/ppermute | solution.py:15
  252.6 9.8 %collective-permute-start.1 = (f32[2,16,1,256]{3,2,1,0:T(1,128)S(1)}, f32[2,16,1,256]{3,2,1,0:T(1,128)S(1)}, u32[]{:S(2)}, u32[]{:S(2)}) collective-permute-start(f32[2,16,1,256]{3,2,1,0:T(1,128)S(1)} %pad_maximum_fusion.11), channel_id=1, source_target_pairs={{1,0},{2,1},{3,2},{4,3},{5,4},{6,5},{7,6},{9,8},{10,9},{11,10},{12... | collective-permute-start | bytes 98312 | tf_op jit(solution)/shard_map/while/body/eval_jaxpr/ppermute | solution.py:15
  254.0 8.5 %collective-permute-start = (f32[2,1,16,256]{3,2,1,0:T(8,128)S(1)}, f32[2,1,16,256]{3,2,1,0:T(8,128)S(1)}, u32[]{:S(2)}, u32[]{:S(2)}) collective-permute-start(f32[2,1,16,256]{3,2,1,0:T(8,128)S(1)} %pad_maximum_fusion.10), channel_id=1, source_target_pairs={{8,0},{16,8},{24,16},{9,1},{17,9},{25,17},{10,2},{18,10},{26,18},{... | collective-permute-start | bytes 98312 | tf_op jit(solution)/shard_map/while/body/eval_jaxpr/ppermute | solution.py:15
  265.5 12.4 %collective-permute-start.2 = (f32[2,16,1,256]{3,2,1,0:T(1,128)S(1)}, f32[2,16,1,256]{3,2,1,0:T(1,128)S(1)}, u32[]{:S(2)}, u32[]{:S(2)}) collective-permute-start(f32[2,16,1,256]{3,2,1,0:T(1,128)S(1)} %pad_maximum_fusion.12), channel_id=1, source_target_pairs={{0,1},{1,2},{2,3},{3,4},{4,5},{5,6},{6,7},{8,9},{9,10},{10,11},{11... | collective-permute-start | bytes 98312 | tf_op jit(solution)/shard_map/while/body/eval_jaxpr/ppermute | solution.py:15
  286.9 9.8 %collective-permute-start.1 = (f32[2,16,1,256]{3,2,1,0:T(1,128)S(1)}, f32[2,16,1,256]{3,2,1,0:T(1,128)S(1)}, u32[]{:S(2)}, u32[]{:S(2)}) collective-permute-start(f32[2,16,1,256]{3,2,1,0:T(1,128)S(1)} %pad_maximum_fusion.11), channel_id=1, source_target_pairs={{1,0},{2,1},{3,2},{4,3},{5,4},{6,5},{7,6},{9,8},{10,9},{11,10},{12... | collective-permute-start | bytes 98312 | tf_op jit(solution)/shard_map/while/body/eval_jaxpr/ppermute | solution.py:15
  288.2 8.5 %collective-permute-start = (f32[2,1,16,256]{3,2,1,0:T(8,128)S(1)}, f32[2,1,16,256]{3,2,1,0:T(8,128)S(1)}, u32[]{:S(2)}, u32[]{:S(2)}) collective-permute-start(f32[2,1,16,256]{3,2,1,0:T(8,128)S(1)} %pad_maximum_fusion.10), channel_id=1, source_target_pairs={{8,0},{16,8},{24,16},{9,1},{17,9},{25,17},{10,2},{18,10},{26,18},{... | collective-permute-start | bytes 98312 | tf_op jit(solution)/shard_map/while/body/eval_jaxpr/ppermute | solution.py:15
  299.8 12.4 %collective-permute-start.2 = (f32[2,16,1,256]{3,2,1,0:T(1,128)S(1)}, f32[2,16,1,256]{3,2,1,0:T(1,128)S(1)}, u32[]{:S(2)}, u32[]{:S(2)}) collective-permute-start(f32[2,16,1,256]{3,2,1,0:T(1,128)S(1)} %pad_maximum_fusion.12), channel_id=1, source_target_pairs={{0,1},{1,2},{2,3},{3,4},{4,5},{5,6},{6,7},{8,9},{9,10},{10,11},{11... | collective-permute-start | bytes 98312 | tf_op jit(solution)/shard_map/while/body/eval_jaxpr/ppermute | solution.py:15
  321.1 9.8 %collective-permute-start.1 = (f32[2,16,1,256]{3,2,1,0:T(1,128)S(1)}, f32[2,16,1,256]{3,2,1,0:T(1,128)S(1)}, u32[]{:S(2)}, u32[]{:S(2)}) collective-permute-start(f32[2,16,1,256]{3,2,1,0:T(1,128)S(1)} %pad_maximum_fusion.11), channel_id=1, source_target_pairs={{1,0},{2,1},{3,2},{4,3},{5,4},{6,5},{7,6},{9,8},{10,9},{11,10},{12... | collective-permute-start | bytes 98312 | tf_op jit(solution)/shard_map/while/body/eval_jaxpr/ppermute | solution.py:15
  322.4 8.5 %collective-permute-start = (f32[2,1,16,256]{3,2,1,0:T(8,128)S(1)}, f32[2,1,16,256]{3,2,1,0:T(8,128)S(1)}, u32[]{:S(2)}, u32[]{:S(2)}) collective-permute-start(f32[2,1,16,256]{3,2,1,0:T(8,128)S(1)} %pad_maximum_fusion.10), channel_id=1, source_target_pairs={{8,0},{16,8},{24,16},{9,1},{17,9},{25,17},{10,2},{18,10},{26,18},{... | collective-permute-start | bytes 98312 | tf_op jit(solution)/shard_map/while/body/eval_jaxpr/ppermute | solution.py:15
  334.0 12.4 %collective-permute-start.2 = (f32[2,16,1,256]{3,2,1,0:T(1,128)S(1)}, f32[2,16,1,256]{3,2,1,0:T(1,128)S(1)}, u32[]{:S(2)}, u32[]{:S(2)}) collective-permute-start(f32[2,16,1,256]{3,2,1,0:T(1,128)S(1)} %pad_maximum_fusion.12), channel_id=1, source_target_pairs={{0,1},{1,2},{2,3},{3,4},{4,5},{5,6},{6,7},{8,9},{9,10},{10,11},{11... | collective-permute-start | bytes 98312 | tf_op jit(solution)/shard_map/while/body/eval_jaxpr/ppermute | solution.py:15
  355.4 9.8 %collective-permute-start.1 = (f32[2,16,1,256]{3,2,1,0:T(1,128)S(1)}, f32[2,16,1,256]{3,2,1,0:T(1,128)S(1)}, u32[]{:S(2)}, u32[]{:S(2)}) collective-permute-start(f32[2,16,1,256]{3,2,1,0:T(1,128)S(1)} %pad_maximum_fusion.11), channel_id=1, source_target_pairs={{1,0},{2,1},{3,2},{4,3},{5,4},{6,5},{7,6},{9,8},{10,9},{11,10},{12... | collective-permute-start | bytes 98312 | tf_op jit(solution)/shard_map/while/body/eval_jaxpr/ppermute | solution.py:15
  356.7 8.5 %collective-permute-start = (f32[2,1,16,256]{3,2,1,0:T(8,128)S(1)}, f32[2,1,16,256]{3,2,1,0:T(8,128)S(1)}, u32[]{:S(2)}, u32[]{:S(2)}) collective-permute-start(f32[2,1,16,256]{3,2,1,0:T(8,128)S(1)} %pad_maximum_fusion.10), channel_id=1, source_target_pairs={{8,0},{16,8},{24,16},{9,1},{17,9},{25,17},{10,2},{18,10},{26,18},{... | collective-permute-start | bytes 98312 | tf_op jit(solution)/shard_map/while/body/eval_jaxpr/ppermute | solution.py:15
  368.3 12.4 %collective-permute-start.2 = (f32[2,16,1,256]{3,2,1,0:T(1,128)S(1)}, f32[2,16,1,256]{3,2,1,0:T(1,128)S(1)}, u32[]{:S(2)}, u32[]{:S(2)}) collective-permute-start(f32[2,16,1,256]{3,2,1,0:T(1,128)S(1)} %pad_maximum_fusion.12), channel_id=1, source_target_pairs={{0,1},{1,2},{2,3},{3,4},{4,5},{5,6},{6,7},{8,9},{9,10},{10,11},{11... | collective-permute-start | bytes 98312 | tf_op jit(solution)/shard_map/while/body/eval_jaxpr/ppermute | solution.py:15
  389.6 9.8 %collective-permute-start.1 = (f32[2,16,1,256]{3,2,1,0:T(1,128)S(1)}, f32[2,16,1,256]{3,2,1,0:T(1,128)S(1)}, u32[]{:S(2)}, u32[]{:S(2)}) collective-permute-start(f32[2,16,1,256]{3,2,1,0:T(1,128)S(1)} %pad_maximum_fusion.11), channel_id=1, source_target_pairs={{1,0},{2,1},{3,2},{4,3},{5,4},{6,5},{7,6},{9,8},{10,9},{11,10},{12... | collective-permute-start | bytes 98312 | tf_op jit(solution)/shard_map/while/body/eval_jaxpr/ppermute | solution.py:15
  390.9 8.5 %collective-permute-start = (f32[2,1,16,256]{3,2,1,0:T(8,128)S(1)}, f32[2,1,16,256]{3,2,1,0:T(8,128)S(1)}, u32[]{:S(2)}, u32[]{:S(2)}) collective-permute-start(f32[2,1,16,256]{3,2,1,0:T(8,128)S(1)} %pad_maximum_fusion.10), channel_id=1, source_target_pairs={{8,0},{16,8},{24,16},{9,1},{17,9},{25,17},{10,2},{18,10},{26,18},{... | collective-permute-start | bytes 98312 | tf_op jit(solution)/shard_map/while/body/eval_jaxpr/ppermute | solution.py:15
  402.5 12.4 %collective-permute-start.2 = (f32[2,16,1,256]{3,2,1,0:T(1,128)S(1)}, f32[2,16,1,256]{3,2,1,0:T(1,128)S(1)}, u32[]{:S(2)}, u32[]{:S(2)}) collective-permute-start(f32[2,16,1,256]{3,2,1,0:T(1,128)S(1)} %pad_maximum_fusion.12), channel_id=1, source_target_pairs={{0,1},{1,2},{2,3},{3,4},{4,5},{5,6},{6,7},{8,9},{9,10},{10,11},{11... | collective-permute-start | bytes 98312 | tf_op jit(solution)/shard_map/while/body/eval_jaxpr/ppermute | solution.py:15
  423.9 9.8 %collective-permute-start.1 = (f32[2,16,1,256]{3,2,1,0:T(1,128)S(1)}, f32[2,16,1,256]{3,2,1,0:T(1,128)S(1)}, u32[]{:S(2)}, u32[]{:S(2)}) collective-permute-start(f32[2,16,1,256]{3,2,1,0:T(1,128)S(1)} %pad_maximum_fusion.11), channel_id=1, source_target_pairs={{1,0},{2,1},{3,2},{4,3},{5,4},{6,5},{7,6},{9,8},{10,9},{11,10},{12... | collective-permute-start | bytes 98312 | tf_op jit(solution)/shard_map/while/body/eval_jaxpr/ppermute | solution.py:15
  425.2 8.5 %collective-permute-start = (f32[2,1,16,256]{3,2,1,0:T(8,128)S(1)}, f32[2,1,16,256]{3,2,1,0:T(8,128)S(1)}, u32[]{:S(2)}, u32[]{:S(2)}) collective-permute-start(f32[2,1,16,256]{3,2,1,0:T(8,128)S(1)} %pad_maximum_fusion.10), channel_id=1, source_target_pairs={{8,0},{16,8},{24,16},{9,1},{17,9},{25,17},{10,2},{18,10},{26,18},{... | collective-permute-start | bytes 98312 | tf_op jit(solution)/shard_map/while/body/eval_jaxpr/ppermute | solution.py:15
  436.8 12.4 %collective-permute-start.2 = (f32[2,16,1,256]{3,2,1,0:T(1,128)S(1)}, f32[2,16,1,256]{3,2,1,0:T(1,128)S(1)}, u32[]{:S(2)}, u32[]{:S(2)}) collective-permute-start(f32[2,16,1,256]{3,2,1,0:T(1,128)S(1)} %pad_maximum_fusion.12), channel_id=1, source_target_pairs={{0,1},{1,2},{2,3},{3,4},{4,5},{5,6},{6,7},{8,9},{9,10},{10,11},{11... | collective-permute-start | bytes 98312 | tf_op jit(solution)/shard_map/while/body/eval_jaxpr/ppermute | solution.py:15
  458.1 9.8 %collective-permute-start.1 = (f32[2,16,1,256]{3,2,1,0:T(1,128)S(1)}, f32[2,16,1,256]{3,2,1,0:T(1,128)S(1)}, u32[]{:S(2)}, u32[]{:S(2)}) collective-permute-start(f32[2,16,1,256]{3,2,1,0:T(1,128)S(1)} %pad_maximum_fusion.11), channel_id=1, source_target_pairs={{1,0},{2,1},{3,2},{4,3},{5,4},{6,5},{7,6},{9,8},{10,9},{11,10},{12... | collective-permute-start | bytes 98312 | tf_op jit(solution)/shard_map/while/body/eval_jaxpr/ppermute | solution.py:15
  459.4 8.5 %collective-permute-start = (f32[2,1,16,256]{3,2,1,0:T(8,128)S(1)}, f32[2,1,16,256]{3,2,1,0:T(8,128)S(1)}, u32[]{:S(2)}, u32[]{:S(2)}) collective-permute-start(f32[2,1,16,256]{3,2,1,0:T(8,128)S(1)} %pad_maximum_fusion.10), channel_id=1, source_target_pairs={{8,0},{16,8},{24,16},{9,1},{17,9},{25,17},{10,2},{18,10},{26,18},{... | collective-permute-start | bytes 98312 | tf_op jit(solution)/shard_map/while/body/eval_jaxpr/ppermute | solution.py:15
  471.0 12.4 %collective-permute-start.2 = (f32[2,16,1,256]{3,2,1,0:T(1,128)S(1)}, f32[2,16,1,256]{3,2,1,0:T(1,128)S(1)}, u32[]{:S(2)}, u32[]{:S(2)}) collective-permute-start(f32[2,16,1,256]{3,2,1,0:T(1,128)S(1)} %pad_maximum_fusion.12), channel_id=1, source_target_pairs={{0,1},{1,2},{2,3},{3,4},{4,5},{5,6},{6,7},{8,9},{9,10},{10,11},{11... | collective-permute-start | bytes 98312 | tf_op jit(solution)/shard_map/while/body/eval_jaxpr/ppermute | solution.py:15
  492.4 9.8 %collective-permute-start.1 = (f32[2,16,1,256]{3,2,1,0:T(1,128)S(1)}, f32[2,16,1,256]{3,2,1,0:T(1,128)S(1)}, u32[]{:S(2)}, u32[]{:S(2)}) collective-permute-start(f32[2,16,1,256]{3,2,1,0:T(1,128)S(1)} %pad_maximum_fusion.11), channel_id=1, source_target_pairs={{1,0},{2,1},{3,2},{4,3},{5,4},{6,5},{7,6},{9,8},{10,9},{11,10},{12... | collective-permute-start | bytes 98312 | tf_op jit(solution)/shard_map/while/body/eval_jaxpr/ppermute | solution.py:15
  505.3 12.4 %collective-permute-start.2 = (f32[2,16,1,256]{3,2,1,0:T(1,128)S(1)}, f32[2,16,1,256]{3,2,1,0:T(1,128)S(1)}, u32[]{:S(2)}, u32[]{:S(2)}) collective-permute-start(f32[2,16,1,256]{3,2,1,0:T(1,128)S(1)} %pad_maximum_fusion.12), channel_id=1, source_target_pairs={{0,1},{1,2},{2,3},{3,4},{4,5},{5,6},{6,7},{8,9},{9,10},{10,11},{11... | collective-permute-start | bytes 98312 | tf_op jit(solution)/shard_map/while/body/eval_jaxpr/ppermute | solution.py:15
  526.6 9.8 %collective-permute-start.1 = (f32[2,16,1,256]{3,2,1,0:T(1,128)S(1)}, f32[2,16,1,256]{3,2,1,0:T(1,128)S(1)}, u32[]{:S(2)}, u32[]{:S(2)}) collective-permute-start(f32[2,16,1,256]{3,2,1,0:T(1,128)S(1)} %pad_maximum_fusion.11), channel_id=1, source_target_pairs={{1,0},{2,1},{3,2},{4,3},{5,4},{6,5},{7,6},{9,8},{10,9},{11,10},{12... | collective-permute-start | bytes 98312 | tf_op jit(solution)/shard_map/while/body/eval_jaxpr/ppermute | solution.py:15
  527.9 8.5 %collective-permute-start = (f32[2,1,16,256]{3,2,1,0:T(8,128)S(1)}, f32[2,1,16,256]{3,2,1,0:T(8,128)S(1)}, u32[]{:S(2)}, u32[]{:S(2)}) collective-permute-start(f32[2,1,16,256]{3,2,1,0:T(8,128)S(1)} %pad_maximum_fusion.10), channel_id=1, source_target_pairs={{8,0},{16,8},{24,16},{9,1},{17,9},{25,17},{10,2},{18,10},{26,18},{... | collective-permute-start | bytes 98312 | tf_op jit(solution)/shard_map/while/body/eval_jaxpr/ppermute | solution.py:15
  539.5 12.4 %collective-permute-start.2 = (f32[2,16,1,256]{3,2,1,0:T(1,128)S(1)}, f32[2,16,1,256]{3,2,1,0:T(1,128)S(1)}, u32[]{:S(2)}, u32[]{:S(2)}) collective-permute-start(f32[2,16,1,256]{3,2,1,0:T(1,128)S(1)} %pad_maximum_fusion.12), channel_id=1, source_target_pairs={{0,1},{1,2},{2,3},{3,4},{4,5},{5,6},{6,7},{8,9},{9,10},{10,11},{11... | collective-permute-start | bytes 98312 | tf_op jit(solution)/shard_map/while/body/eval_jaxpr/ppermute | solution.py:15
  (442 other events, 2429.8 us)
Sparse Core Ops, SparseCore 0:
  562.9 58.8 all-gather.2
